TPU v7x, 32 devices: a whole 2x2x4 slice. The times are simulated.
32 devices in a mesh: rep: 16 (over z, y, core), tp: 2 (over x).
Axes of the slice: x: 2, y: 2, z: 4, core: 2. Of those that a mesh axis runs over, the one named last changes fastest.
Arguments:
- activations: bfloat16 [8192, 6144], P('rep', 'tp'), may hold values from -6 to 6
- norm_gain: float32 [6144], replicated, may hold values from 0.5 to 1.5
- query_gain: float32 [128], replicated, may hold values from 0.5 to 18
- key_gain: float32 [128], replicated, may hold values from 0.5 to 18
- project_in: bfloat16 [6144, 24, 384], P('rep', 'tp'), may hold values from -1 to 1
- project_out: bfloat16 [6144, 3072], P('rep', 'tp'), may hold values from -1 to 1
Outputs:
- attended: bfloat16 [8192, 6144], P('rep', 'tp')
- weight_norms: float32 [2], replicated
All inputs are finite; a program needn't handle non-finite values.
Results may differ from a plain program's by a relative error of at most 0.018.
The roundings to bfloat16 on the way count: a program that leaves them out, or rounds other values in their place, can miss the bound.
Values may be sent and summed in bfloat16 or wider, within the bound.
A program may use at most 192 MiB of HBM per device.

v0:
```python
import math

import jax
import jax.numpy as jnp
from jax import lax
from jax.sharding import PartitionSpec as P

D = 6144
HEADS = 24
HEAD_DIM = 128
PATCHES = 256


def layer_norm(values, gain):
    average = jnp.mean(values, -1, keepdims=True)
    centred = values - average
    variance = jnp.mean(centred * centred, -1, keepdims=True)
    return centred * lax.rsqrt(variance + 1e-06) * gain


def shards(activations, norm_gain, query_gain, key_gain, project_in, project_out):
    gathered_rows = lax.all_gather(activations, "tp", axis=1, tiled=True)
    normed = layer_norm(gathered_rows.astype(jnp.float32), norm_gain).astype(jnp.bfloat16)
    tok_rows = normed.shape[0]
    local_heads = project_in.shape[1]
    head_dim = project_in.shape[2] // 3
    piece = lax.all_gather(project_in, "rep", axis=0, tiled=True)
    running = jnp.dot(normed, piece.reshape(piece.shape[0], -1), preferred_element_type=jnp.float32)
    projected = running
    images_here = tok_rows // PATCHES
    projected = projected.reshape(images_here, PATCHES, local_heads, 3 * head_dim)
    queries = layer_norm(projected[..., :head_dim], query_gain).astype(jnp.bfloat16)
    keys_normed = layer_norm(projected[..., head_dim : 2 * head_dim], key_gain).astype(jnp.bfloat16)
    values = projected[..., 2 * head_dim :].astype(jnp.bfloat16)
    scores = jnp.einsum(
        "iphd,iqhd->ihpq", queries, keys_normed, preferred_element_type=jnp.float32
    ) / math.sqrt(head_dim)
    probabilities = jax.nn.softmax(scores, axis=-1).astype(jnp.bfloat16)
    mixed = jnp.einsum("ihpq,iqhd->iphd", probabilities, values, preferred_element_type=jnp.float32)
    mixed = mixed.astype(jnp.bfloat16).reshape(tok_rows, local_heads * head_dim)
    product = lax.dot_general(
        mixed,
        lax.all_gather(project_out, "rep", axis=0, tiled=True),
        (((1,), (1,)), ((), ())),
        preferred_element_type=jnp.float32,
    )
    attended = lax.psum_scatter(product.astype(jnp.bfloat16), "tp", scatter_dimension=1, tiled=True)
    local_in = jnp.sum(jnp.square(project_in.astype(jnp.float32)))
    local_out = jnp.sum(jnp.square(project_out.astype(jnp.float32)))
    total_in, total_out = lax.psum((local_in, local_out), ("rep", "tp"))
    weight_norms = jnp.stack([jnp.sqrt(total_in / (3 * HEADS * HEAD_DIM)), jnp.sqrt(total_out / D)])
    return (attended, weight_norms)


def solution(mesh):
    in_specs = (P("rep", "tp"), P(), P(), P(), P("rep", "tp", None), P("rep", "tp"))
    out_specs = (P("rep", "tp"), P())
    return jax.shard_map(shards, mesh=mesh, in_specs=in_specs, out_specs=out_specs, check_vma=False)
```

profile of v0, /device:TPU:0, one launch (start us, length us, event | category | flops | bytes accessed | tf_op | source)
XLA Modules:
  0.0 571.8 jit_solution(6341764529476445264)
XLA Ops:
  7.2 0.7 all-gather.4.cloned.1.call-update
  7.9 6.0 %copy.10 = bf16[384,12,384]{0,2,1:T(8,128)(2,1)} copy(bf16[384,12,384]{2,0,1:T(8,128)(2,1)} %param.10) | data formatting | bytes 7077888 | tf_op args[4]
  14.1 0.7 all-gather.8.cloned.1.call-update
  14.8 77.8 %all-gather.4.cloned.1.call-done = bf16[512,6144]{1,0:T(8,128)(2,1)} async-done(((bf16[512,3072]{1,0:T(8,128)(2,1)}), bf16[512,6144]{1,0:T(8,128)(2,1)}) %all-gather.4.cloned.1.call-update) | async-done | bytes 6291472 | tf_op jit(solution)/shard_map/all_gather | solution.py:22
  92.6 3.8 convert_reduce_fusion
  96.5 0.7 copy-done
  97.2 1.8 fusion.5
  99.0 6.3 %fusion.7 = bf16[512,6144]{1,0:T(8,128)(2,1)} fusion(bf16[512,6144]{1,0:T(8,128)(2,1)S(1)} %copy-done, f32[6144]{0:T(1024)S(1)} %copy-done.3, f32[512]{0:T(512)S(1)} %add_rsqrt_fusion.2, f32[512]{0:T(512)S(1)} %broadcast_multiply_fusion.2), kind=kLoop, calls=%fused_computation.9 | loop fusion | flops 15728640 | bytes 12611584 | tf_op jit(solution)/shard_map/convert_element_type | solution.py:23
  105.3 265.2 %all-gather.6.cloned.1.call-done = bf16[6144,12,384]{0,2,1:T(8,128)(2,1)} async-done(((bf16[384,12,384]{0,2,1:T(8,128)(2,1)}), bf16[6144,12,384]{0,2,1:T(8,128)(2,1)}) %all-gather.6.cloned.1.call-update) | async-done | bytes 56623120 | tf_op jit(solution)/shard_map/all_gather | solution.py:27
  370.5 37.1 %fusion.1 = f32[2,256,12,384]{3,1,2,0:T(8,128)} fusion(bf16[2,256,6144,1]{2,1,3,0:T(8,128)(2,1)} %bitcast.26, bf16[6144,12,384]{0,2,1:T(8,128)(2,1)} %all-gather.6.cloned.1.call-done), kind=kOutput, calls=%fused_computation.1 | convolution fusion | flops 28991029248 | bytes 72351744 | tf_op jit(solution)/shard_map/dot_general | solution.py:28
  407.6 4.7 slice_reduce_fusion.1
  412.4 5.8 %multiply_reduce_fusion.3 = (f32[2,256,12]{1,2,0:T(8,128)S(1)}, f32[2,256,12]{1,2,0:T(8,128)S(1)}) fusion(f32[2,256,12,384]{3,1,2,0:T(8,128)} %fusion.1, f32[2,256,12]{1,2,0:T(8,128)S(1)} %get-tuple-element.11, f32[2,256,12]{1,2,0:T(8,128)S(1)} %get-tuple-element.10), kind=kLoop, calls=%fused_computation.21 | loop fusion | flops 4706304 | bytes 6389760 | tf_op jit(solution)/shard_map/reduce_sum | solution.py:17
  418.3 3.5 fusion.14
  421.8 5.0 fusion.23
  426.8 0.9 fusion.21
  427.7 1.6 copy.13
  429.7 41.3 %all-gather.8.cloned.1.call-done = bf16[6144,1536]{1,0:T(8,128)(2,1)} async-done(((bf16[384,1536]{1,0:T(8,128)(2,1)}), bf16[6144,1536]{1,0:T(8,128)(2,1)}) %all-gather.8.cloned.1.call-update) | async-done | bytes 18874384 | tf_op jit(solution)/shard_map/all_gather | solution.py:43
  471.0 15.6 %convolution_convert_fusion = bf16[512,6144]{1,0:T(8,128)(2,1)} fusion(bf16[512,1536]{0,1:T(8,128)(2,1)S(1)} %bitcast.28, bf16[6144,1536]{1,0:T(8,128)(2,1)} %all-gather.8.cloned.1.call-done), kind=kOutput, calls=%fused_computation.10 | convolution fusion | flops 9666822144 | bytes 26738688 | tf_op jit(solution)/shard_map/dot_general | solution.py:41
  486.6 2.0 copy-done.2
  488.6 2.4 multiply_reduce_fusion
  491.0 2.5 multiply_reduce_fusion.4
  493.5 41.4 %all-reduce = (f32[]{:T(128)}, f32[]{:T(128)}) all-reduce(f32[]{:T(128)} %multiply_reduce_fusion.4, f32[]{:T(128)} %multiply_reduce_fusion), channel_id=1, replica_groups=mesh['rep'=16,'tp'=2] {'rep','tp'}, use_global_device_ids=true, to_apply=%region_12.0 | all-reduce | flops 2 | bytes 16 | tf_op jit(solution)/shard_map/psum | solution.py:50
  536.2 0.6 pad_maximum_fusion
  536.8 28.5 %reduce-scatter.2.cloned.1.call-done = bf16[512,3072]{1,0:T(8,128)(2,1)} async-done(((bf16[512,6144]{1,0:T(8,128)(2,1)}), bf16[512,3072]{1,0:T(8,128)(2,1)}) %reduce-scatter.2.cloned.1.call-update) | async-done | bytes 3145744 | tf_op jit(solution)/shard_map/reduce_scatter | solution.py:47
  (22 shorter events, 0.6 us)
Async XLA Ops:
  7.2 85.5 %all-gather.4.cloned.1.call-start = ((), (), s32[]{:S(2)}) async-start(), calls=%async_computation.1 | async-start | bytes 9437184 | tf_op jit(solution)/shard_map/all_gather | solution.py:22
  7.9 362.6 %all-gather.6.cloned.1.call-start = ((), (), s32[]{:S(2)}) async-start(), calls=%async_computation.2 | async-start | bytes 60162048 | tf_op jit(solution)/shard_map/all_gather | solution.py:27
  14.0 457.0 %all-gather.8.cloned.1.call-start = ((), (), s32[]{:S(2)}) async-start(), calls=%async_computation.3 | async-start | bytes 20054016 | tf_op jit(solution)/shard_map/all_gather | solution.py:43
  14.1 85.0 %copy-start.3 = (f32[6144]{0:T(1024)S(1)}, f32[6144]{0:T(1024)}, u32[]{:S(2)}) copy-start(f32[6144]{0:T(1024)} %param.7) | copy-start | bytes 73732
  14.7 550.6 %reduce-scatter.2.cloned.1.call-start = ((), (), s32[]{:S(2)}) async-start(), calls=%async_computation.4 | async-start | bytes 9437184 | tf_op jit(solution)/shard_map/reduce_scatter | solution.py:47
  92.6 4.6 copy-start
  407.6 10.6 %copy-start.1 = (f32[2,256,12,384]{3,1,2,0:T(8,128)S(1)}, f32[2,256,12,384]{3,1,2,0:T(8,128)}, u32[]{:S(2)}) copy-start(f32[2,256,12,384]{3,1,2,0:T(8,128)} %fusion.1) | copy-start | bytes 28311556
  407.6 10.6 %copy-start.4 = (f32[128]{0:T(128)S(1)}, f32[128]{0:T(128)}, u32[]{:S(2)}) copy-start(f32[128]{0:T(128)} %param.9) | copy-start | bytes 1540
  407.6 10.6 %copy-start.5 = (f32[128]{0:T(128)S(1)}, f32[128]{0:T(128)}, u32[]{:S(2)}) copy-start(f32[128]{0:T(128)} %param.8) | copy-start | bytes 1540
  486.6 2.0 copy-start.2
Sparse Core Ops, SparseCore 0:
  9.5 83.0 all-gather.3
  94.2 276.2 all-gather.5
  372.1 98.8 all-gather.7
  486.8 78.5 reduce-scatter.1
where the time goes:
time: 572 us
  waiting for transfers between devices  414 us (72%)
  matrix products  57.2 us (10%)
  blocking collectives  41.4 us (7%)
  other arithmetic  33 us (6%)
  between operations  15.2 us (3%)
  local copies, waits for them, and re-layouts  10.7 us (2%)
    all_gather x1, waiting for transfers between devices, shards(): piece = lax.all_gather(project_in, 'rep', axis=0, tiled=True)  265 us
    all_gather x1, waiting for transfers between devices, shards(): gathered_rows = lax.all_gather(activations, 'tp', axis=1, tiled=True)  77.8 us
    psum x1, blocking collectives, shards(): total_in, total_out = lax.psum((local_in, local_out), ('rep', 'tp'))  41.4 us
    all_gather x1, waiting for transfers between devices, shards(): lax.all_gather(project_out, 'rep', axis=0, tiled=True)  41.3 us
    dot_general x1, matrix products, shards(): jnp.dot(normed, piece.reshape(piece.shape[0], -1), preferred_element_type...  37.1 us
    reduce_scatter x1, waiting for transfers between devices, shards(): lax.psum_scatter(product.astype(jnp.bfloat16), 'tp', scatter_dimension=1,...  28.5 us
    dot_general x1, matrix products, shards(): lax.dot_general(mixed, lax.all_gather(project_out, 'rep', axis=0, tiled=T...  15.6 us
  transfers between devices with their start and end apart: 4, of which 4 were waited for; matrix products, arithmetic and copies ran while one was open for 14% of the time, Pallas kernels for 0%

commit v1 on v0

v1 whole, which is shorter than its diff:
```python
import functools
import math

import jax
import jax.numpy as jnp
from jax import lax
from jax.sharding import PartitionSpec as P

D = 6144
HEADS = 24
HEAD_DIM = 128
PATCHES = 256


def layer_norm(values, gain):
    average = jnp.mean(values, -1, keepdims=True)
    centred = values - average
    variance = jnp.mean(centred * centred, -1, keepdims=True)
    return centred * lax.rsqrt(variance + 1e-06) * gain


def heads_mixed(projected, query_gain, key_gain, head_dim):
    tok_rows, width = projected.shape
    heads = width // (3 * head_dim)
    projected = projected.reshape(tok_rows // PATCHES, PATCHES, heads, 3 * head_dim)
    queries = layer_norm(projected[..., :head_dim], query_gain).astype(jnp.bfloat16)
    keys_normed = layer_norm(projected[..., head_dim : 2 * head_dim], key_gain).astype(jnp.bfloat16)
    values = projected[..., 2 * head_dim :].astype(jnp.bfloat16)
    scores = jnp.einsum(
        "iphd,iqhd->ihpq", queries, keys_normed, preferred_element_type=jnp.float32
    ) / math.sqrt(head_dim)
    probabilities = jax.nn.softmax(scores, axis=-1).astype(jnp.bfloat16)
    mixed = jnp.einsum("ihpq,iqhd->iphd", probabilities, values, preferred_element_type=jnp.float32)
    return mixed.astype(jnp.bfloat16).reshape(tok_rows, heads * head_dim)


def chunk_count(size, wanted):
    while size % wanted:
        wanted -= 1
    return wanted


def shards(n_rep, n_tp, activations, norm_gain, query_gain, key_gain, project_in, project_out):
    me = lax.axis_index("tp")
    swap = [(0, 1), (1, 0)]
    local_rows, local_heads, head_width = project_in.shape
    head_dim = head_width // 3

    n_in = chunk_count(local_heads, 3)
    step = local_heads // n_in
    pieces = []
    for j in range(n_in):
        part = project_in[:, j * step : (j + 1) * step].reshape(local_rows, step * head_width)
        pieces.append(lax.all_gather(part, "rep", axis=0, tiled=True))
    out_rows, out_depth = project_out.shape
    n_out = chunk_count(out_rows // 128, 3) if out_rows % 128 == 0 else 1
    span = out_rows // n_out
    out_pieces = []
    for j in range(n_out):
        part = project_out[j * span : (j + 1) * span]
        out_pieces.append(lax.all_gather(part, "rep", axis=0, tiled=True))

    local_in = jnp.sum(jnp.square(project_in.astype(jnp.float32)))
    local_out = jnp.sum(jnp.square(project_out.astype(jnp.float32)))
    totals = lax.psum(jnp.stack([local_in, local_out]), ("rep", "tp"))
    if n_tp == 2:
        other = lax.ppermute(activations, "tp", swap)
        other, totals = lax.optimization_barrier((other, totals))
        first = jnp.where(me == 0, activations, other)
        second = jnp.where(me == 0, other, activations)
        gathered_rows = jnp.concatenate([first, second], axis=1)
    else:
        gathered_rows = lax.all_gather(activations, "tp", axis=1, tiled=True)
    normed = layer_norm(gathered_rows.astype(jnp.float32), norm_gain).astype(jnp.bfloat16)

    mixed = []
    for piece in pieces:
        projected = jnp.dot(normed, piece, preferred_element_type=jnp.float32)
        mixed.append(heads_mixed(projected, query_gain, key_gain, head_dim))
    mixed = jnp.concatenate(mixed, axis=1)

    def product(rows):
        total = lax.dot_general(
            mixed, rows, (((1,), (1,)), ((), ())), preferred_element_type=jnp.float32
        )
        return total.astype(jnp.bfloat16)

    sums = []
    for piece in out_pieces:
        if n_tp == 2:
            half = piece.shape[0] // 2
            sent = product(lax.dynamic_slice_in_dim(piece, (1 - me) * half, half, 0))
            arrived = lax.ppermute(sent, "tp", swap)
            kept = product(lax.dynamic_slice_in_dim(piece, me * half, half, 0))
            total = kept.astype(jnp.float32) + arrived.astype(jnp.float32)
            sums.append(total.astype(jnp.bfloat16))
        else:
            sums.append(lax.psum_scatter(product(piece), "tp", scatter_dimension=1, tiled=True))
    owners = n_rep // n_tp
    blocks = [sums[j][:, r * span : (r + 1) * span] for r in range(owners) for j in range(n_out)]
    attended = jnp.concatenate(blocks, axis=1)
    fans = jnp.array([3 * HEADS * HEAD_DIM, D], jnp.float32)
    return (attended, jnp.sqrt(totals / fans))


def solution(mesh):
    in_specs = (P("rep", "tp"), P(), P(), P(), P("rep", "tp", None), P("rep", "tp"))
    out_specs = (P("rep", "tp"), P())
    body = functools.partial(shards, mesh.shape["rep"], mesh.shape["tp"])
    return jax.shard_map(body, mesh=mesh, in_specs=in_specs, out_specs=out_specs, check_vma=False)
```

time: 572 us -> 548 us (0.958)
  waiting for transfers between devices: 414 us -> 246 us
  blocking collectives: 41.4 us -> 98.2 us
  local copies, waits for them, and re-layouts: 10.7 us -> 50.6 us
  matrix products: 57.2 us -> 89.1 us
  starting transfers between devices: 0.16 us -> 7.74 us
    all_gather x3 -> x6, waiting for transfers between devices: 384 us -> 229 us  [the longest x3 139 us: shards(): out_pieces.append(lax.all_gather(part, 'rep', axis=0, tiled=True))]
    psum x1, blocking collectives: 41.4 us -> 98.2 us  [shards(): totals = lax.psum(jnp.stack([local_in, local_out]), ('rep', 'tp'))]
    dot_general x4 -> x15, matrix products: 57.2 us -> 89.1 us  [the longest x3 50.8 us: shards(): projected = jnp.dot(normed, piece, preferred_element_type=jnp.float32)]
    reduce_scatter x1 -> x0, waiting for transfers between devices: 28.5 us -> none  [shards(): lax.psum_scatter(product.astype(jnp.bfloat16), 'tp', scatter_dimension=1,...]
    ppermute x0 -> x4, waiting for transfers between devices: none -> 16.8 us  [the longest x3 16.8 us: shards(): arrived = lax.ppermute(sent, 'tp', swap)]
    unnamed x14 -> x73, local copies, waits for them, and re-layouts: 9.11 us -> 22.8 us
    reshape x0 -> x3, local copies, waits for them, and re-layouts: none -> 12.9 us  [heads_mixed(): projected.reshape(tok_rows // PATCHES, PATCHES, heads, 3 * head_dim)]
    slice x0 -> x5, local copies, waits for them, and re-layouts: none -> 10.3 us  [the longest x3 5.44 us: heads_mixed(): values = projected[..., 2 * head_dim:].astype(jnp.bfloat16)]
  transfers between devices with their start and end apart: 4 -> 10, of which waited for: 4 -> 6; matrix products, arithmetic and copies ran while one was open for 14% -> 30% of each run, Pallas kernels for 0% -> 0%
where the time goes in v1:
time: 548 us; the launch traced here: 544 us
  waiting for transfers between devices  246 us (45%)
  blocking collectives  98.2 us (18%)
  matrix products  89.1 us (16%)
  local copies, waits for them, and re-layouts  50.6 us (9%)
  other arithmetic  36.9 us (7%)
  between operations  14.9 us (3%)
  starting transfers between devices  7.74 us (1%)
    all_gather x3, waiting for transfers between devices, shards(): out_pieces.append(lax.all_gather(part, 'rep', axis=0, tiled=True))  139 us
    psum x1, blocking collectives, shards(): totals = lax.psum(jnp.stack([local_in, local_out]), ('rep', 'tp'))  98.2 us
    all_gather x3, waiting for transfers between devices, shards(): pieces.append(lax.all_gather(part, 'rep', axis=0, tiled=True))  89.7 us
    dot_general x3, matrix products, shards(): projected = jnp.dot(normed, piece, preferred_element_type=jnp.float32)  50.8 us
    unnamed x73, local copies, waits for them, and re-layouts  22.8 us
    dot_general x6, matrix products, product(): lax.dot_general(mixed, rows, (((1,), (1,)), ((), ())), preferred_element_...  22 us
    ppermute x3, waiting for transfers between devices, shards(): arrived = lax.ppermute(sent, 'tp', swap)  16.8 us
    reduce_sum x6, other arithmetic, layer_norm(): variance = jnp.mean(centred * centred, -1, keepdims=True)  14.3 us
  transfers between devices with their start and end apart: 10, of which 6 were waited for; matrix products, arithmetic and copies ran while one was open for 30% of the time, Pallas kernels for 0%

profile of v1, /device:TPU:0, one launch (start us, length us, event | category | flops | bytes accessed | tf_op | source)
XLA Modules:
  0.0 543.6 jit_solution(12540614699131464713)
XLA Ops:
  26.8 98.2 %psum.7 = f32[2]{0:T(128)S(1)} all-reduce(f32[2]{0:T(128)S(1)} %pad_maximum_fusion.1), channel_id=1, replica_groups=mesh['rep'=16,'tp'=2] {'rep','tp'}, use_global_device_ids=true, to_apply=%region_2.0 | all-reduce | flops 2 | bytes 16 | tf_op jit(solution)/shard_map/psum | solution.py:65
  125.0 3.3 broadcast_select_fusion.1
  129.9 4.1 fusion.5
  134.1 16.9 %fusion.109 = f32[512,1536]{1,0:T(8,128)} fusion(bf16[6144,1536]{0,1:T(8,128)(2,1)} %all-gather.9.cloned.1.call-done, f32[6144]{0:T(1024)S(1)} %copy-done.12, f32[512]{0:T(512)S(1)} %add_rsqrt_fusion.6, f32[512]{0:T(512)S(1)} %broadcast_multiply_fusion.6, bf16[512,3072]{1,0:T(8,128)(2,1)} %copy-done, bf16[512,3072]{1,0:T(8,128)(2,1)S(1)} %get-tuple-element.12), kind=kOutput, calls=%fused_computation.164 | convolution fusion | flops 9688842240 | bytes 28340224 | tf_op jit(solution)/shard_map/dot_general | solution.py:78
  151.0 4.8 reshape.128
  155.8 58.2 %all-gather.11.cloned.1.call-done = bf16[6144,1536]{0,1:T(8,128)(2,1)} async-done(((bf16[384,1536]{0,1:T(8,128)(2,1)}), bf16[6144,1536]{0,1:T(8,128)(2,1)}) %all-gather.11.cloned.1.call-update) | async-done | bytes 18874384 | tf_op jit(solution)/shard_map/all_gather | solution.py:54
  214.0 17.3 %fusion.107 = f32[512,1536]{1,0:T(8,128)} fusion(bf16[6144,1536]{0,1:T(8,128)(2,1)} %all-gather.11.cloned.1.call-done, f32[6144]{0:T(1024)S(1)} %copy-done.12, f32[512]{0:T(512)S(1)} %add_rsqrt_fusion.6, f32[512]{0:T(512)S(1)} %broadcast_multiply_fusion.6, bf16[512,3072]{1,0:T(8,128)(2,1)} %copy-done, bf16[512,3072]{1,0:T(8,128)(2,1)S(1)} %get-tuple-element.12), kind=kOutput, calls=%fused_computation.163 | convolution fusion | flops 9688842240 | bytes 28340224 | tf_op jit(solution)/shard_map/dot_general | solution.py:78
  231.3 4.9 reshape.131
  236.2 6.6 %slice_reduce_fusion.1 = (f32[2,256,4]{2,1,0:T(8,128)}, f32[2,256,4]{2,1,0:T(8,128)}, f32[2,256,4,128]{3,2,1,0:T(4,128)}, f32[2,256,4,128]{3,2,1,0:T(4,128)}, f3...) fusion(f32[2,256,4,384]{3,2,1,0:T(4,128)} %reshape.131, ...), kind=kLoop, calls=%fused_computation.158 | loop fusion | flops 1040384 | bytes 8421376 | tf_op jit(solution)/shard_map/reduce_sum | solution.py:16
  260.1 3.5 fusion.49
  277.4 3.4 fusion.48
  282.9 31.5 %all-gather.7.cloned.1.call-done = bf16[6144,1536]{0,1:T(8,128)(2,1)} async-done(((bf16[384,1536]{0,1:T(8,128)(2,1)}), bf16[6144,1536]{0,1:T(8,128)(2,1)}) %all-gather.7.cloned.1.call-update) | async-done | bytes 18874384 | tf_op jit(solution)/shard_map/all_gather | solution.py:54
  314.4 16.6 %fusion.111 = f32[512,1536]{1,0:T(8,128)} fusion(bf16[6144,1536]{0,1:T(8,128)(2,1)} %all-gather.7.cloned.1.call-done, f32[6144]{0:T(1024)S(1)} %copy-done.12, f32[512]{0:T(512)S(1)} %add_rsqrt_fusion.6, f32[512]{0:T(512)S(1)} %broadcast_multiply_fusion.6, bf16[512,3072]{1,0:T(8,128)(2,1)} %copy-done, bf16[512,3072]{1,0:T(8,128)(2,1)S(1)} %get-tuple-element.12), kind=kOutput, calls=%fused_computation.165 | convolution fusion | flops 9688842240 | bytes 28340224 | tf_op jit(solution)/shard_map/dot_general | solution.py:78
  331.0 3.2 reshape.125
  335.2 3.1 slice_reduce_fusion.5
  350.5 27.4 %all-gather.13.cloned.1.call-done = bf16[2048,1536]{1,0:T(8,128)(2,1)} async-done(((bf16[128,1536]{1,0:T(8,128)(2,1)}), bf16[2048,1536]{1,0:T(8,128)(2,1)}) %all-gather.13.cloned.1.call-update) | async-done | bytes 6291472 | tf_op jit(solution)/shard_map/all_gather | solution.py:61
  377.9 4.7 fusion.26
  384.6 55.6 %all-gather.15.cloned.1.call-done = bf16[2048,1536]{1,0:T(8,128)(2,1)} async-done(((bf16[128,1536]{1,0:T(8,128)(2,1)}), bf16[2048,1536]{1,0:T(8,128)(2,1)}) %all-gather.15.cloned.1.call-update) | async-done | bytes 6291472 | tf_op jit(solution)/shard_map/all_gather | solution.py:61
  440.2 4.7 fusion.32
  446.4 56.1 %all-gather.17.cloned.1.call-done = bf16[2048,1536]{1,0:T(8,128)(2,1)} async-done(((bf16[128,1536]{1,0:T(8,128)(2,1)}), bf16[2048,1536]{1,0:T(8,128)(2,1)}) %all-gather.17.cloned.1.call-update) | async-done | bytes 6291472 | tf_op jit(solution)/shard_map/all_gather | solution.py:61
  502.5 3.9 fusion.38
  507.9 3.7 add_convert_fusion.2
  511.7 3.2 add_convert_fusion.1
  515.0 16.7 %collective-permute-done.3 = bf16[512,1024]{1,0:T(8,128)(2,1)S(1)} collective-permute-done((bf16[512,1024]{1,0:T(8,128)(2,1)S(1)}, bf16[512,1024]{1,0:T(8,128)(2,1)S(1)}, u32[]{:S(2)}, u32[]{:S(2)}) %collective-permute-start.3) | collective-permute-done | bytes 1048608 | tf_op jit(solution)/shard_map/ppermute | solution.py:93
  (137 shorter events, 77.1 us)
Async XLA Ops:
  7.2 126.9 %all-gather.9.cloned.1.call-start = ((), (), s32[]{:S(2)}) async-start(), calls=%async_computation.1 | async-start | bytes 20054016 | tf_op jit(solution)/shard_map/all_gather | solution.py:54
  11.1 202.9 %all-gather.11.cloned.1.call-start = ((), (), s32[]{:S(2)}) async-start(), calls=%async_computation.2 | async-start | bytes 20054016 | tf_op jit(solution)/shard_map/all_gather | solution.py:54
  12.7 301.7 %all-gather.7.cloned.1.call-start = ((), (), s32[]{:S(2)}) async-start(), calls=%async_computation | async-start | bytes 20054016 | tf_op jit(solution)/shard_map/all_gather | solution.py:54
  14.2 8.8 %copy-start.1 = (bf16[384,12,384]{2,0,1:T(8,128)(2,1)S(1)}, bf16[384,12,384]{2,0,1:T(8,128)(2,1)}, u32[]{:S(2)}) copy-start(bf16[384,12,384]{2,0,1:T(8,128)(2,1)} %param.11) | copy-start | bytes 10616836
  14.2 363.7 %all-gather.13.cloned.1.call-start = ((), (), s32[]{:S(2)}) async-start(), calls=%async_computation.3 | async-start | bytes 6684672 | tf_op jit(solution)/shard_map/all_gather | solution.py:61
  16.7 423.5 %all-gather.15.cloned.1.call-start = ((), (), s32[]{:S(2)}) async-start(), calls=%async_computation.4 | async-start | bytes 6684672 | tf_op jit(solution)/shard_map/all_gather | solution.py:61
  17.3 485.1 %all-gather.17.cloned.1.call-start = ((), (), s32[]{:S(2)}) async-start(), calls=%async_computation.5 | async-start | bytes 6684672 | tf_op jit(solution)/shard_map/all_gather | solution.py:61
  17.4 107.6 %collective-permute-start = (bf16[512,3072]{1,0:T(8,128)(2,1)}, bf16[512,3072]{1,0:T(8,128)(2,1)}, u32[]{:S(2)}, u32[]{:S(2)}) collective-permute-start(bf16[512,3072]{1,0:T(8,128)(2,1)} %param.7), channel_id=1, source_target_pairs={{0,1},{1,0},{2,3},{3,2},{4,5},{5,4},{6,7},{7,6},{8,9},{9,8},{10,11... | collective-permute-start | bytes 9437192 | tf_op jit(solution)/shard_map/ppermute | solution.py:67
  128.3 1.7 copy-start
  129.9 4.2 copy-start.12
  242.8 12.4 %copy-start.10 = (f32[128]{0:T(128)S(1)}, f32[128]{0:T(128)}, u32[]{:S(2)}) copy-start(f32[128]{0:T(128)} %param.10) | copy-start | bytes 1540
  242.8 12.5 %copy-start.11 = (f32[128]{0:T(128)S(1)}, f32[128]{0:T(128)}, u32[]{:S(2)}) copy-start(f32[128]{0:T(128)} %param.9) | copy-start | bytes 1540
  338.3 5.4 copy-start.2
  338.3 5.4 copy-start.3
  347.0 2.8 copy-start.8
  350.5 33.5 %copy-start.13 = (f32[2]{0:T(128)S(1)}, f32[2]{0:T(128)}, u32[]{:S(2)}) copy-start(f32[2]{0:T(128)} %constant.46) | copy-start | bytes 28
  382.6 125.3 %collective-permute-start.1 = (bf16[512,1024]{1,0:T(8,128)(2,1)}, bf16[512,1024]{1,0:T(8,128)(2,1)S(1)}, u32[]{:S(2)}, u32[]{:S(2)}) collective-permute-start(bf16[512,1024]{1,0:T(8,128)(2,1)} %fusion.26), channel_id=1, source_target_pairs={{0,1},{1,0},{2,3},{3,2},{4,5},{5,4},{6,7},{7,6},{8,9},{9,8},{10,11... | collective-permute-start | bytes 3145736 | tf_op jit(solution)/shard_map/ppermute | solution.py:93
  444.9 66.7 %collective-permute-start.2 = (bf16[512,1024]{1,0:T(8,128)(2,1)}, bf16[512,1024]{1,0:T(8,128)(2,1)}, u32[]{:S(2)}, u32[]{:S(2)}) collective-permute-start(bf16[512,1024]{1,0:T(8,128)(2,1)} %fusion.32), channel_id=1, source_target_pairs={{0,1},{1,0},{2,3},{3,2},{4,5},{5,4},{6,7},{7,6},{8,9},{9,8},{10,11... | collective-permute-start | bytes 3145736 | tf_op jit(solution)/shard_map/ppermute | solution.py:93
  502.5 9.2 %slice-start = ((s8[6291456]{0:T(1024)(128)(4,1)}), s8[4194304]{0:T(1024)(128)(4,1)S(1)}, s32[]{:S(2)}) async-start(s8[6291456]{0:T(1024)(128)(4,1)} %bitcast.41), calls=%async_computation.6 | async-start | bytes 8388608
  506.3 5.3 slice-start.1
  506.3 25.4 %collective-permute-start.3 = (bf16[512,1024]{1,0:T(8,128)(2,1)S(1)}, bf16[512,1024]{1,0:T(8,128)(2,1)S(1)}, u32[]{:S(2)}, u32[]{:S(2)}) collective-permute-start(bf16[512,1024]{1,0:T(8,128)(2,1)S(1)} %fusion.38), channel_id=1, source_target_pairs={{0,1},{1,0},{2,3},{3,2},{4,5},{5,4},{6,7},{7,6},{8,9},{9,8},{10,11... | collective-permute-start | bytes 3145736 | tf_op jit(solution)/shard_map/ppermute | solution.py:93
  511.6 20.1 %slice-start.2 = ((s8[6291456]{0:T(1024)(128)(4,1)}), s8[4194304]{0:T(1024)(128)(4,1)S(1)}, s32[]{:S(2)}) async-start(s8[6291456]{0:T(1024)(128)(4,1)} %bitcast.43), calls=%async_computation.8 | async-start | bytes 8388608
  511.6 20.1 %slice-start.3 = ((s8[6291456]{0:T(1024)(128)(4,1)}), s8[2097152]{0:T(1024)(128)(4,1)S(1)}, s32[]{:S(2)}) async-start(s8[6291456]{0:T(1024)(128)(4,1)} %bitcast.43), calls=%async_computation.9 | async-start | bytes 4194304
  534.8 1.7 copy-start.9
  (4 other events, 5.0 us)
Sparse Core Ops, SparseCore 0:
  11.2 102.4 all-gather.8
  115.3 98.7 all-gather.10
  215.6 98.7 all-gather.6
  316.5 61.3 all-gather.12
  380.0 60.0 all-gather.14
  442.3 60.0 all-gather.16
